TPU v7x, 32 devices: a whole 2x2x4 slice. The times are simulated.
32 devices in a mesh: replica: 2 (over x), tp: 8 (over z, y), sub: 2 (over core).
Axes of the slice: x: 2, y: 2, z: 4, core: 2. Of those that a mesh axis runs over, the one named last changes fastest.
Arguments:
- hidden_in: bfloat16 [8, 8192], P('replica'), parts along dimension 0, may hold values from -6 to 6
- norm_gain: float32 [16384], P('replica'), parts along dimension 0, may hold values from 0.1 to 1.9
- wqkv_old: bfloat16 [16, 2, 1280, 4096], P(('replica', 'tp'), 'sub'), parts along dimension 0, may hold values from -0.1875 to 0.1875
- wo: bfloat16 [16384, 8192], P(('replica', 'tp', 'sub')), parts along dimension 0, may hold values from -0.0625 to 0.0625
- key_cache: bfloat16 [8, 4096, 1024], P('replica', ('tp', 'sub')), parts along dimension 0, may hold values from -240 to 240
- value_cache: bfloat16 [8, 4096, 1024], P('replica', ('tp', 'sub')), parts along dimension 0, may hold values from -6 to 6
- lengths: int32 [8], P('replica'), parts along dimension 0, may hold values from 1 to 4096
- section_order: int32 [32], P('replica'), parts along dimension 0, may hold values from 0 to 15, each once
Outputs:
- mixed_out: bfloat16 [8, 8192], P('replica'), parts along dimension 0
- wqkv_new: bfloat16 [16, 2, 640, 8192], P(('replica', 'tp'), 'sub'), parts along dimension 0
There are 2 independent parts, one for each index of `replica`. A program takes and returns all parts, laid end to end along the dimension named above; each array names one. Nothing has to cross between parts.
Inputs may be any that keep to these rules, and one draw needn't show every extreme that they name: `section_order`: each input row block appears once. The new token's position is lengths[b].
All inputs are finite; a program needn't handle non-finite values.
Results may differ from a plain program's by a relative error of at most 0.0085.
The roundings to bfloat16 on the way count: a program that leaves them out, or rounds other values in their place, can miss the bound.
Values may be sent and summed in bfloat16 or wider, within the bound.
A program may use at most 128 MiB of HBM per device.

v0:
```python
import math

import jax
import jax.numpy as jnp
from jax import lax
from jax.experimental import pallas as pl
from jax.experimental.pallas import tpu as pltpu
from jax.sharding import PartitionSpec as P

HEADS = 64
KV_HEADS = 8
HEAD_DIM = 128
RANKS = 8
ROW_BLOCKS = 16
PER_SECTION_TP = 4
CHUNK_ROWS = 16
AHEAD = 4
MESH = pl.DeviceIdType.MESH
CONTRACT_LAST = (((1,), (1,)), ((), ()))


def layer_kernel(
    sections,
    hidden_in,
    gain_in,
    w_in,
    wo_in,
    key_in,
    value_in,
    lengths_in,
    order_in,
    mixed_out,
    new_out,
    hidden,
    gain,
    weight,
    held,
    wo,
    keys,
    values,
    lengths,
    order,
    places,
    normed,
    own_rows,
    x1,
    units,
    raw,
    turned,
    own_q,
    new_k,
    new_v,
    mask,
    mixes,
    parts,
    x2,
    merged,
    x3,
    attended,
    shares,
    x4,
    x5,
    x6,
    moved,
    load_sems,
    bulk_send,
    bulk_recv,
    cross_send,
    cross_recv,
    side_send,
    side_recv,
):
    members = RANKS
    replica = lax.axis_index("replica")
    tp = lax.axis_index("tp")
    sub = lax.axis_index("sub")
    section = tp // PER_SECTION_TP
    column = lax.rem(tp, PER_SECTION_TP)
    member = column * 2 + sub
    rank = section * members + member

    seqs, width = hidden.shape
    cols_dev = held.shape[1]
    rows_old = held.shape[2]
    per_section = ROW_BLOCKS // sections
    block_rows = rows_old // per_section
    unit_count = weight.shape[0]
    positions = keys.shape[1]
    own_heads = own_q.shape[1] // seqs
    head_rows = own_heads * seqs
    chunk_count = cols_dev // CHUNK_ROWS
    piece_count = chunk_count * (sections - 1)
    inverse = 1.0 / math.sqrt(HEAD_DIM)
    groups = HEADS // KV_HEADS
    share = width // members

    def cross_peer(off):
        other = lax.rem(section + off, sections)
        return other, (replica, other * PER_SECTION_TP + column, sub)

    def side_peer(off):
        other = lax.rem(member + off, members)
        return other, (replica, section * PER_SECTION_TP + other // 2, lax.rem(other, 2))

    barrier = pltpu.get_barrier_semaphore()
    for off in range(1, sections):
        pl.semaphore_signal(barrier, inc=1, device_id=cross_peer(off)[1], device_id_type=MESH)
    for off in range(1, members):
        pl.semaphore_signal(barrier, inc=1, device_id=side_peer(off)[1], device_id_type=MESH)

    own_start = pl.multiple_of(section * cols_dev, CHUNK_ROWS)
    loads = [
        pltpu.make_async_copy(source, target, load_sems.at[index])
        for index, (source, target) in enumerate(
            (
                (hidden_in, hidden),
                (gain_in, gain),
                (order_in, order),
                (lengths_in, lengths),
                (w_in.at[0, 0], weight),
                (key_in, keys),
                (value_in, values),
                (wo_in, wo),
                (w_in.at[0, 0, pl.ds(own_start, cols_dev)], held.at[section]),
            )
        )
    ]
    for load in loads:
        load.start()
    pl.semaphore_wait(barrier, sections - 1 + members - 1)

    def piece(index, arriving):
        chunk = index // (sections - 1)
        off = lax.rem(index, sections - 1) + 1
        other, peer = cross_peer(off)
        start = pl.multiple_of(chunk * CHUNK_ROWS, CHUNK_ROWS)
        slot = lax.rem(section + sections - off, sections) if arriving else section
        return pltpu.make_async_remote_copy(
            src_ref=w_in.at[
                0, 0, pl.ds(pl.multiple_of(other * cols_dev + start, CHUNK_ROWS), CHUNK_ROWS)
            ],
            dst_ref=held.at[slot, pl.ds(start, CHUNK_ROWS)],
            send_sem=bulk_send.at[index],
            recv_sem=bulk_recv.at[index],
            device_id=peer,
            device_id_type=MESH,
        )

    queued = [0]

    def queue(count):
        first = queued[0]
        last = min(first + count, piece_count)
        queued[0] = last
        if last > first:
            lax.fori_loop(first, last, lambda index, _: piece(index, False).start(), None)

    sent = []

    def cross_swap(step, source_of, target):
        def copy(off, arriving):
            other, peer = cross_peer(off)
            slot = lax.rem(section + sections - off, sections) if arriving else section
            return pltpu.make_async_remote_copy(
                src_ref=source_of(other),
                dst_ref=target.at[slot],
                send_sem=cross_send.at[step, off - 1],
                recv_sem=cross_recv.at[step, off - 1],
                device_id=peer,
                device_id_type=MESH,
            )

        for off in range(1, sections):
            outgoing = copy(off, False)
            outgoing.start()
            sent.append(outgoing)
        return lambda: [copy(off, True).wait_recv() for off in range(1, sections)]

    def side_swap(step, source_of, target):
        def copy(off, arriving):
            other, peer = side_peer(off)
            slot = lax.rem(member + members - off, members) if arriving else member
            return pltpu.make_async_remote_copy(
                src_ref=source_of(other),
                dst_ref=target.at[slot],
                send_sem=side_send.at[step, off - 1],
                recv_sem=side_recv.at[step, off - 1],
                device_id=peer,
                device_id_type=MESH,
            )

        for off in range(1, members):
            outgoing = copy(off, False)
            outgoing.start()
            sent.append(outgoing)
        return lambda: [copy(off, True).wait_recv() for off in range(1, members)]

    queue(AHEAD)

    for load in loads[:4]:
        load.wait()
    widened = hidden[...].astype(jnp.float32)
    factor = lax.rsqrt(jnp.mean(widened * widened, -1, keepdims=True) + 1e-05)
    rounded = (widened * factor * gain[...]).astype(jnp.bfloat16).astype(jnp.float32)
    for block in range(ROW_BLOCKS):
        normed[block] = rounded[:, block * block_rows : (block + 1) * block_rows]
    for slot in range(per_section):
        own_rows[:, slot * block_rows : (slot + 1) * block_rows] = normed[
            order[section * per_section + slot]
        ]
    loads[4].wait()
    rows = own_rows[...].astype(jnp.bfloat16)
    tile = 256

    def project(step, _):
        start = pl.multiple_of(step * tile, tile)
        x1[section, :, pl.ds(start, tile)] = lax.dot_general(
            rows, weight[pl.ds(start, tile), :], CONTRACT_LAST, preferred_element_type=jnp.float32
        )

    lax.fori_loop(0, unit_count // tile, project, None)
    arrive = cross_swap(0, lambda other: x1.at[section], x1)
    queue(AHEAD)

    row_index = lax.broadcasted_iota(jnp.int32, (8, HEAD_DIM), 0)
    lane_index = lax.broadcasted_iota(jnp.int32, (8, HEAD_DIM), 1)

    def by_seq(seq_of_row):
        picked = jnp.full(seq_of_row.shape, lengths[0], jnp.int32)
        for seq in range(1, seqs):
            picked = jnp.where(seq_of_row == seq, lengths[seq], picked)
        return picked

    half = HEAD_DIM // 2
    pair = jnp.where(lane_index < half, lane_index, lane_index - half).astype(jnp.float32)
    freqs = jnp.exp(pair * (-2.0 * math.log(500000.0) / HEAD_DIM))
    angles = by_seq(lax.rem(row_index, seqs)).astype(jnp.float32) * freqs
    cosine = jnp.cos(angles)
    sine = jnp.where(lane_index < half, -jnp.sin(angles), jnp.sin(angles))

    wide = (groups * seqs, seqs * positions)
    seq_of_row = lax.rem(lax.broadcasted_iota(jnp.int32, wide, 0), seqs)
    at = lax.broadcasted_iota(jnp.int32, wide, 1)
    usable = (at // positions == seq_of_row) & (
        rank * positions + lax.rem(at, positions) < by_seq(seq_of_row)
    )
    mask[...] = jnp.where(usable, 1.0, 0.0)

    def find(block, _):
        place = jnp.int32(0)
        for old in range(ROW_BLOCKS):
            place = jnp.where(order[old] == block, old, place)
        places[block] = place

    lax.fori_loop(0, ROW_BLOCKS, find, None)

    arrive()
    total = x1[0]
    for other in range(1, sections):
        total = total + x1[other]
    units[member] = total.astype(jnp.bfloat16).astype(jnp.float32)
    arrive = side_swap(0, lambda other: units.at[member], units)
    queue(AHEAD)
    for load in loads[5:]:
        load.wait()
    arrive()

    per_rank = unit_count // HEAD_DIM
    for head in range(HEADS + 2 * KV_HEADS):
        lane = (head % per_rank) * HEAD_DIM
        raw[head * seqs : (head + 1) * seqs, :] = units[
            head // per_rank, :, lane : lane + HEAD_DIM
        ]

    def turn(step, _):
        start = pl.multiple_of(step * 8, 8)
        vectors = raw[pl.ds(start, 8), :]
        out = vectors * cosine + pltpu.roll(vectors, half, 1) * sine
        turned[pl.ds(start, 8), :] = out.astype(jnp.bfloat16).astype(jnp.float32)

    lax.fori_loop(0, (HEADS + KV_HEADS) * seqs // 8, turn, None)
    for owner in range(sections * members):
        own_q[owner] = turned[owner * head_rows : (owner + 1) * head_rows, :]
    for head in range(KV_HEADS):
        key_row = (HEADS + head) * seqs
        value_row = (HEADS + KV_HEADS + head) * seqs
        for copy in range(own_heads):
            new_k[head, copy * seqs : (copy + 1) * seqs, :] = turned[key_row : key_row + seqs, :]
            new_v[head, copy * seqs : (copy + 1) * seqs, :] = raw[value_row : value_row + seqs, :]

    owners = groups // own_heads
    stat_lane = lax.broadcasted_iota(jnp.int32, (groups * seqs, HEAD_DIM), 1)

    def attend(head, _):
        lane = pl.ds(pl.multiple_of(head * HEAD_DIM, HEAD_DIM), HEAD_DIM)
        row = pl.multiple_of(head * groups * seqs, groups * seqs)
        query = turned[pl.ds(row, groups * seqs), :].astype(jnp.bfloat16)
        key = keys[:, :, lane].reshape(seqs * positions, HEAD_DIM)
        value = values[:, :, lane].reshape(seqs * positions, HEAD_DIM)
        open_ = mask[...] > 0.5
        scores = (
            lax.dot_general(query, key, CONTRACT_LAST, preferred_element_type=jnp.float32)
            * inverse
        )
        top = jnp.max(jnp.where(open_, scores, -1e30), -1, keepdims=True)
        weights = jnp.exp(jnp.where(open_, scores - top, -1e30))
        summed = jnp.sum(weights, -1, keepdims=True)
        high = weights.astype(jnp.bfloat16)
        low = (weights - high.astype(jnp.float32)).astype(jnp.bfloat16)
        mixes[:, :HEAD_DIM] = jnp.dot(
            high, value, preferred_element_type=jnp.float32
        ) + jnp.dot(low, value, preferred_element_type=jnp.float32)
        mixes[:, HEAD_DIM:] = jnp.where(stat_lane < half, top, summed)
        for index in range(owners):
            owner = head * owners + index
            parts[lax.rem(owner, members), owner // members] = mixes[
                index * head_rows : (index + 1) * head_rows, :
            ]

    lax.fori_loop(0, KV_HEADS, attend, None)
    arrive = side_swap(1, lambda other: parts.at[other], x2)
    x2[member] = parts[member]
    queue(AHEAD)
    arrive()

    def combined(refs):
        best = refs[0][:, HEAD_DIM : HEAD_DIM + 1]
        for ref in refs[1:]:
            best = jnp.maximum(best, ref[:, HEAD_DIM : HEAD_DIM + 1])
        mix = jnp.zeros((head_rows, HEAD_DIM), jnp.float32)
        summed = jnp.zeros((head_rows, 1), jnp.float32)
        for ref in refs:
            scale = jnp.exp(ref[:, HEAD_DIM : HEAD_DIM + 1] - best)
            mix = mix + ref[:, :HEAD_DIM] * scale
            summed = summed + ref[:, HEAD_DIM + half : HEAD_DIM + half + 1] * scale
        return best, summed, mix

    own_lane = lax.broadcasted_iota(jnp.int32, (head_rows, HEAD_DIM), 1)
    for other in range(sections):
        best, summed, mix = combined([x2[source, other] for source in range(members)])
        merged[other, :, :HEAD_DIM] = mix
        merged[other, :, HEAD_DIM:] = jnp.where(own_lane < half, best, summed)
    arrive = cross_swap(1, lambda other: merged.at[other], x3)
    x3[section] = merged[section]
    queue(AHEAD)
    arrive()

    best, summed, mix = combined([x3[source] for source in range(sections)])
    kv_head = rank * own_heads // groups
    own_score = jnp.sum(own_q[rank] * new_k[kv_head], -1, keepdims=True) * inverse
    highest = jnp.maximum(best, own_score)
    old_scale = jnp.exp(best - highest)
    own_weight = jnp.exp(own_score - highest)
    numerator = mix * old_scale + own_weight * new_v[kv_head]
    denominator = summed * old_scale + own_weight
    attended[...] = numerator / denominator
    flat = jnp.concatenate(
        [attended[head * seqs : (head + 1) * seqs, :] for head in range(own_heads)], -1
    ).astype(jnp.bfloat16)

    def give(other, _):
        lane = pl.ds(pl.multiple_of(other * share, share), share)
        shares[other] = jnp.dot(flat, wo[:, lane], preferred_element_type=jnp.float32)

    lax.fori_loop(0, members, give, None)
    arrive = side_swap(2, lambda other: shares.at[other], x4)
    x4[member] = shares[member]
    queue(AHEAD)
    arrive()

    total = x4[0]
    for other in range(1, members):
        total = total + x4[other]
    x5[section] = total
    arrive = cross_swap(2, lambda other: x5.at[section], x5)
    queue(AHEAD)
    arrive()

    total = hidden[:, pl.ds(pl.multiple_of(member * share, share), share)].astype(jnp.float32)
    product = x5[0]
    for other in range(1, sections):
        product = product + x5[other]
    x6[member] = (total + product).astype(jnp.bfloat16).astype(jnp.float32)
    arrive = side_swap(3, lambda other: x6.at[member], x6)
    queue(piece_count)
    arrive()
    for other in range(members):
        mixed_out[:, other * share : (other + 1) * share] = x6[other].astype(jnp.bfloat16)

    def place(chunk, _):
        for off in range(1, sections):
            piece(chunk * (sections - 1) + off - 1, True).wait_recv()
        start = pl.multiple_of(chunk * CHUNK_ROWS, CHUNK_ROWS)
        for old in range(ROW_BLOCKS):
            first = old % per_section * block_rows
            moved[old] = held[
                old // per_section, pl.ds(start, CHUNK_ROWS), first : first + block_rows
            ]
        for block in range(ROW_BLOCKS):
            new_out[0, 0, pl.ds(start, CHUNK_ROWS), block * block_rows : (block + 1) * block_rows] = (
                moved[places[block]]
            )

    lax.fori_loop(0, chunk_count, place, None)

    for outgoing in sent:
        outgoing.wait_send()
    lax.fori_loop(0, piece_count, lambda index, _: piece(index, False).wait_send(), None)


def shards(hidden_in, norm_gain, wqkv_old, wo, key_cache, value_cache, lengths, section_order):
    sections = lax.axis_size("tp") // PER_SECTION_TP
    members = PER_SECTION_TP * lax.axis_size("sub")
    seqs, width = hidden_in.shape
    unit_count, rows_old = wqkv_old.shape[2:]
    cols_dev = unit_count // sections
    block_rows = width // ROW_BLOCKS
    positions = key_cache.shape[1]
    own_heads = wo.shape[0] // HEAD_DIM
    head_rows = own_heads * seqs
    share = width // members
    pieces = cols_dev // CHUNK_ROWS * (sections - 1)
    f32, bf16 = jnp.float32, jnp.bfloat16
    heads = HEADS + 2 * KV_HEADS

    def kernel(*refs):
        layer_kernel(sections, *refs)

    scratch = [
        pltpu.VMEM(hidden_in.shape, bf16),
        pltpu.VMEM((1, width), f32),
        pltpu.VMEM((unit_count, rows_old), bf16),
        pltpu.VMEM((sections, cols_dev, rows_old), bf16),
        pltpu.VMEM(wo.shape, bf16),
        pltpu.VMEM(key_cache.shape, bf16),
        pltpu.VMEM(value_cache.shape, bf16),
        pltpu.SMEM(lengths.shape, jnp.int32),
        pltpu.SMEM(section_order.shape, jnp.int32),
        pltpu.SMEM(section_order.shape, jnp.int32),
        pltpu.VMEM((ROW_BLOCKS, seqs, block_rows), f32),
        pltpu.VMEM((seqs, rows_old), f32),
        pltpu.VMEM((sections, seqs, unit_count), f32),
        pltpu.VMEM((members, seqs, unit_count), f32),
        pltpu.VMEM((heads * seqs, HEAD_DIM), f32),
        pltpu.VMEM((heads * seqs, HEAD_DIM), f32),
        pltpu.VMEM((sections * members, head_rows, HEAD_DIM), f32),
        pltpu.VMEM((KV_HEADS, head_rows, HEAD_DIM), f32),
        pltpu.VMEM((KV_HEADS, head_rows, HEAD_DIM), f32),
        pltpu.VMEM((HEADS // KV_HEADS * seqs, seqs * positions), f32),
        pltpu.VMEM((HEADS // KV_HEADS * seqs, 2 * HEAD_DIM), f32),
        pltpu.VMEM((members, sections, head_rows, 2 * HEAD_DIM), f32),
        pltpu.VMEM((members, sections, head_rows, 2 * HEAD_DIM), f32),
        pltpu.VMEM((sections, head_rows, 2 * HEAD_DIM), f32),
        pltpu.VMEM((sections, head_rows, 2 * HEAD_DIM), f32),
        pltpu.VMEM((head_rows, HEAD_DIM), f32),
        pltpu.VMEM((members, seqs, share), f32),
        pltpu.VMEM((members, seqs, share), f32),
        pltpu.VMEM((sections, seqs, share), f32),
        pltpu.VMEM((members, seqs, share), f32),
        pltpu.VMEM((ROW_BLOCKS, CHUNK_ROWS, block_rows), bf16),
        pltpu.SemaphoreType.DMA((9,)),
        pltpu.SemaphoreType.DMA((pieces,)),
        pltpu.SemaphoreType.DMA((pieces,)),
        pltpu.SemaphoreType.DMA((3, sections - 1)),
        pltpu.SemaphoreType.DMA((3, sections - 1)),
        pltpu.SemaphoreType.DMA((4, members - 1)),
        pltpu.SemaphoreType.DMA((4, members - 1)),
    ]
    with jax.named_scope("layer"):
        return pl.pallas_call(
            kernel,
            out_shape=(
                pltpu.VMEM((seqs, width), bf16),
                pltpu.VMEM((1, 1, cols_dev, width), bf16),
            ),
            in_specs=[pl.BlockSpec(memory_space=pltpu.HBM)] * 8,
            out_specs=(pl.BlockSpec(memory_space=pltpu.VMEM), pl.BlockSpec(memory_space=pltpu.VMEM)),
            scratch_shapes=scratch,
            compiler_params=pltpu.CompilerParams(
                collective_id=0, has_side_effects=True, vmem_limit_bytes=45 * 2**20
            ),
        )(
            hidden_in,
            norm_gain.reshape(1, width),
            wqkv_old,
            wo,
            key_cache,
            value_cache,
            lengths,
            section_order,
        )


def solution(mesh):
    placed = (
        P("replica", None),
        P("replica"),
        P(("replica", "tp"), "sub", None, None),
        P(("replica", "tp", "sub"), None),
        P("replica", ("tp", "sub"), None),
        P("replica", ("tp", "sub"), None),
        P("replica"),
        P("replica"),
    )
    return jax.shard_map(
        shards,
        mesh=mesh,
        in_specs=placed,
        out_specs=(P("replica", None), P(("replica", "tp"), "sub", None, None)),
        check_vma=False,
    )
```

profile of v0, /device:TPU:27, one launch (start us, length us, event | category | flops | bytes accessed | tf_op | source)
XLA Modules:
  0.0 237.3 jit_solution(18327899386169755719)
XLA Ops:
  0.6 232.0 %layer.1 = (bf16[4,8192]{1,0:T(4,128)(2,1)S(1)}, bf16[1,1,640,8192]{3,2,1,0:T(8,128)(2,1)S(1)}) custom-call(bf16[4,8192]{1,0:T(4,128)(2,1)} %refs_0_.1, f32[1,8192]{1,0:T(1,128)} %bitcast.1, bf16[1,1,1280,4096]{3,2,1,0:T(8,128)(2,1)} %refs_2_.1, bf16[512,8192]{1,0:T(8,128)(2,1)} %refs_3_.1, bf16[4,256,1024]{2,1,0:T(8,128)(2,1)} %refs_4_.1, ...), custom_call_target="tpu_custom_call" | custom-call | tf_op jit(solution)/shard_map/layer/pallas_call | solution.py:470
  232.6 0.6 copy.12
  233.3 4.1 %copy.13 = bf16[1,1,640,8192]{3,2,1,0:T(8,128)(2,1)} copy(bf16[1,1,640,8192]{3,2,1,0:T(8,128)(2,1)S(1)} %get-tuple-element.3) | data formatting | bytes 20971520
where the time goes:
time: 242 us; the launch traced here: 237 us
  Pallas kernels  232 us (96%)
  local copies, waits for them, and re-layouts  4.72 us (2%)
    pallas_call x1, Pallas kernels, shards(): pl.pallas_call(kernel, out_shape=(pltpu.VMEM((seqs, width), bf16), pltpu....  232 us

commit v1 on v0

--- a/solution.py
+++ b/solution.py
@@ -14,7 +14,7 @@
 ROW_BLOCKS = 16
 PER_SECTION_TP = 4
 CHUNK_ROWS = 16
-AHEAD = 4
+AHEAD = 6
 MESH = pl.DeviceIdType.MESH
 CONTRACT_LAST = (((1,), (1,)), ((), ()))
 
@@ -69,6 +69,7 @@
     cross_recv,
     side_send,
     side_recv,
+    section_in,
 ):
     members = RANKS
     replica = lax.axis_index("replica")
@@ -103,10 +104,16 @@
         return other, (replica, section * PER_SECTION_TP + other // 2, lax.rem(other, 2))
 
     barrier = pltpu.get_barrier_semaphore()
+    lower = members // 2
+    in_lower = member < lower
     for off in range(1, sections):
         pl.semaphore_signal(barrier, inc=1, device_id=cross_peer(off)[1], device_id_type=MESH)
     for off in range(1, members):
-        pl.semaphore_signal(barrier, inc=1, device_id=side_peer(off)[1], device_id_type=MESH)
+        other, peer = side_peer(off)
+
+        @pl.when(other < lower)
+        def _():
+            pl.semaphore_signal(barrier, inc=1, device_id=peer, device_id_type=MESH)
 
     own_start = pl.multiple_of(section * cols_dev, CHUNK_ROWS)
     loads = [
@@ -127,7 +134,13 @@
     ]
     for load in loads:
         load.start()
-    pl.semaphore_wait(barrier, sections - 1 + members - 1)
+    pl.semaphore_wait(barrier, sections - 1 + jnp.where(in_lower, members - 1, 0))
+
+    @pl.when(in_lower)
+    def _():
+        pl.semaphore_signal(
+            section_in, inc=1, device_id=side_peer(lower)[1], device_id_type=MESH
+        )
 
     def piece(index, arriving):
         chunk = index // (sections - 1)
@@ -259,6 +272,11 @@
     for other in range(1, sections):
         total = total + x1[other]
     units[member] = total.astype(jnp.bfloat16).astype(jnp.float32)
+
+    @pl.when(jnp.logical_not(in_lower))
+    def _():
+        pl.semaphore_wait(section_in, 1)
+
     arrive = side_swap(0, lambda other: units.at[member], units)
     queue(AHEAD)
     for load in loads[5:]:
@@ -465,6 +483,7 @@
         pltpu.SemaphoreType.DMA((3, sections - 1)),
         pltpu.SemaphoreType.DMA((4, members - 1)),
         pltpu.SemaphoreType.DMA((4, members - 1)),
+        pltpu.SemaphoreType.REGULAR,
     ]
     with jax.named_scope("layer"):
         return pl.pallas_call(

time: 242 us -> 240 us (level)
  no operation moved by 1% of the time
where the time goes in v1:
time: 240 us; the launch traced here: 237 us
  Pallas kernels  232 us (97%)
  local copies, waits for them, and re-layouts  4.72 us (2%)
    pallas_call x1, Pallas kernels, shards(): pl.pallas_call(kernel, out_shape=(pltpu.VMEM((seqs, width), bf16), pltpu....  232 us

profile of v1, /device:TPU:27, one launch (start us, length us, event | category | flops | bytes accessed | tf_op | source)
XLA Modules:
  0.0 237.4 jit_solution(996276241882651109)
XLA Ops:
  0.6 232.0 %layer.1 = (bf16[4,8192]{1,0:T(4,128)(2,1)S(1)}, bf16[1,1,640,8192]{3,2,1,0:T(8,128)(2,1)S(1)}) custom-call(bf16[4,8192]{1,0:T(4,128)(2,1)} %refs_0_.1, f32[1,8192]{1,0:T(1,128)} %bitcast.1, bf16[1,1,1280,4096]{3,2,1,0:T(8,128)(2,1)} %refs_2_.1, bf16[512,8192]{1,0:T(8,128)(2,1)} %refs_3_.1, bf16[4,256,1024]{2,1,0:T(8,128)(2,1)} %refs_4_.1, ...), custom_call_target="tpu_custom_call" | custom-call | tf_op jit(solution)/shard_map/layer/pallas_call | solution.py:489
  232.6 0.6 copy.12
  233.3 4.1 %copy.13 = bf16[1,1,640,8192]{3,2,1,0:T(8,128)(2,1)} copy(bf16[1,1,640,8192]{3,2,1,0:T(8,128)(2,1)S(1)} %get-tuple-element.3) | data formatting | bytes 20971520

commit v2 on v0

--- a/solution.py
+++ b/solution.py
@@ -15,6 +15,7 @@
 PER_SECTION_TP = 4
 CHUNK_ROWS = 16
 AHEAD = 4
+WRITES = 4
 MESH = pl.DeviceIdType.MESH
 CONTRACT_LAST = (((1,), (1,)), ((), ()))
 
@@ -69,6 +70,7 @@
     cross_recv,
     side_send,
     side_recv,
+    section_in,
 ):
     members = RANKS
     replica = lax.axis_index("replica")
@@ -103,10 +105,18 @@
         return other, (replica, section * PER_SECTION_TP + other // 2, lax.rem(other, 2))
 
     barrier = pltpu.get_barrier_semaphore()
+    is_first = member == 0
     for off in range(1, sections):
         pl.semaphore_signal(barrier, inc=1, device_id=cross_peer(off)[1], device_id_type=MESH)
-    for off in range(1, members):
-        pl.semaphore_signal(barrier, inc=1, device_id=side_peer(off)[1], device_id_type=MESH)
+
+    @pl.when(jnp.logical_not(is_first))
+    def _():
+        pl.semaphore_signal(
+            barrier,
+            inc=1,
+            device_id=(replica, section * PER_SECTION_TP, 0),
+            device_id_type=MESH,
+        )
 
     own_start = pl.multiple_of(section * cols_dev, CHUNK_ROWS)
     loads = [
@@ -127,7 +137,14 @@
     ]
     for load in loads:
         load.start()
-    pl.semaphore_wait(barrier, sections - 1 + members - 1)
+    pl.semaphore_wait(barrier, sections - 1 + jnp.where(is_first, members - 1, 0))
+
+    @pl.when(is_first)
+    def _():
+        for off in range(1, members):
+            pl.semaphore_signal(
+                section_in, inc=1, device_id=side_peer(off)[1], device_id_type=MESH
+            )
 
     def piece(index, arriving):
         chunk = index // (sections - 1)
@@ -259,6 +276,11 @@
     for other in range(1, sections):
         total = total + x1[other]
     units[member] = total.astype(jnp.bfloat16).astype(jnp.float32)
+
+    @pl.when(jnp.logical_not(is_first))
+    def _():
+        pl.semaphore_wait(section_in, 1)
+
     arrive = side_swap(0, lambda other: units.at[member], units)
     queue(AHEAD)
     for load in loads[5:]:
@@ -406,6 +428,37 @@
     for outgoing in sent:
         outgoing.wait_send()
     lax.fori_loop(0, piece_count, lambda index, _: piece(index, False).wait_send(), None)
+
+
+def written(mixed, new_weight):
+    rows = new_weight.shape[2] // WRITES
+
+    def kernel(mixed_ref, new_ref, mixed_out, new_out, sems):
+        copies = [pltpu.make_async_copy(mixed_ref, mixed_out, sems.at[WRITES])]
+        for index in range(WRITES):
+            part = (0, 0, pl.ds(index * rows, rows))
+            copies.append(
+                pltpu.make_async_copy(new_ref.at[part], new_out.at[part], sems.at[index])
+            )
+        for copy in copies:
+            copy.start()
+        for copy in copies:
+            copy.wait()
+
+    return pl.pallas_call(
+        kernel,
+        out_shape=(
+            jax.ShapeDtypeStruct(mixed.shape, mixed.dtype),
+            jax.ShapeDtypeStruct(new_weight.shape, new_weight.dtype),
+        ),
+        in_specs=[pl.BlockSpec(memory_space=pltpu.VMEM)] * 2,
+        out_specs=(pl.BlockSpec(memory_space=pltpu.HBM), pl.BlockSpec(memory_space=pltpu.HBM)),
+        scratch_shapes=[pltpu.SemaphoreType.DMA((WRITES + 1,))],
+        compiler_params=pltpu.CompilerParams(vmem_limit_bytes=2**20),
+    )(
+        pltpu.with_memory_space_constraint(mixed, pltpu.VMEM),
+        pltpu.with_memory_space_constraint(new_weight, pltpu.VMEM),
+    )
 
 
 def shards(hidden_in, norm_gain, wqkv_old, wo, key_cache, value_cache, lengths, section_order):
@@ -465,9 +518,10 @@
         pltpu.SemaphoreType.DMA((3, sections - 1)),
         pltpu.SemaphoreType.DMA((4, members - 1)),
         pltpu.SemaphoreType.DMA((4, members - 1)),
+        pltpu.SemaphoreType.REGULAR,
     ]
     with jax.named_scope("layer"):
-        return pl.pallas_call(
+        results = pl.pallas_call(
             kernel,
             out_shape=(
                 pltpu.VMEM((seqs, width), bf16),
@@ -489,6 +543,8 @@
             lengths,
             section_order,
         )
+    with jax.named_scope("written"):
+        return written(*results)
 
 
 def solution(mesh):

time: 242 us -> 239 us (0.988); the launches traced: 237 us -> 237 us
  local copies, waits for them, and re-layouts: 4.72 us -> 0 us
  Pallas kernels: 232 us -> 236 us
    unnamed x2 -> x0, local copies, waits for them, and re-layouts: 4.72 us -> none
    pallas_call x0 -> x1, Pallas kernels: none -> 4.07 us  [written(): pl.pallas_call(kernel, out_shape=(jax.ShapeDtypeStruct(mixed.shape, mixed...]
where the time goes in v2:
time: 239 us; the launch traced here: 237 us
  Pallas kernels  236 us (99%)
    pallas_call x1, Pallas kernels, shards(): pl.pallas_call(kernel, out_shape=(pltpu.VMEM((seqs, width), bf16), pltpu....  232 us

profile of v2, /device:TPU:27, one launch (start us, length us, event | category | flops | bytes accessed | tf_op | source)
XLA Modules:
  0.0 237.1 jit_solution(9440381813624551349)
XLA Ops:
  0.6 232.4 %layer.1 = (bf16[4,8192]{1,0:T(4,128)(2,1)S(1)}, bf16[1,1,640,8192]{3,2,1,0:T(8,128)(2,1)S(1)}) custom-call(bf16[4,8192]{1,0:T(4,128)(2,1)} %refs_0_.1, f32[1,8192]{1,0:T(1,128)} %bitcast.1, bf16[1,1,1280,4096]{3,2,1,0:T(8,128)(2,1)} %refs_2_.1, bf16[512,8192]{1,0:T(8,128)(2,1)} %refs_3_.1, bf16[4,256,1024]{2,1,0:T(8,128)(2,1)} %refs_4_.1, ...), custom_call_target="tpu_custom_call" | custom-call | tf_op jit(solution)/shard_map/layer/pallas_call | solution.py:524
  233.0 4.1 %written.1 = (bf16[4,8192]{1,0:T(4,128)(2,1)}, bf16[1,1,640,8192]{3,2,1,0:T(8,128)(2,1)}) custom-call(bf16[4,8192]{1,0:T(4,128)(2,1)S(1)} %get-tuple-element.4.mixed_ref, bf16[1,1,640,8192]{3,2,1,0:T(8,128)(2,1)S(1)} %get-tuple-element.5.new_ref), custom_call_target="tpu_custom_call" | custom-call | tf_op jit(solution)/shard_map/written/pallas_call | solution.py:448

commit v3 on v2

--- a/solution.py
+++ b/solution.py
@@ -15,9 +15,16 @@
 PER_SECTION_TP = 4
 CHUNK_ROWS = 16
 AHEAD = 4
-WRITES = 4
+EARLY_TENTHS = 7
+LEAD = 2
+HOLD = 4
+TRIGGER = 1
 MESH = pl.DeviceIdType.MESH
 CONTRACT_LAST = (((1,), (1,)), ((), ()))
+
+
+def early_count(chunk_count):
+    return max(1, chunk_count * EARLY_TENTHS // 10)
 
 
 def layer_kernel(
@@ -91,6 +98,10 @@
     own_heads = own_q.shape[1] // seqs
     head_rows = own_heads * seqs
     chunk_count = cols_dev // CHUNK_ROWS
+    early_chunks = early_count(chunk_count)
+    late = column >= PER_SECTION_TP // 2
+    chunks_here = jnp.where(late, early_chunks, chunk_count)
+    early_pieces = early_chunks * (sections - 1)
     piece_count = chunk_count * (sections - 1)
     inverse = 1.0 / math.sqrt(HEAD_DIM)
     groups = HEADS // KV_HEADS
@@ -167,7 +178,7 @@
 
     def queue(count):
         first = queued[0]
-        last = min(first + count, piece_count)
+        last = min(first + count, early_pieces)
         queued[0] = last
         if last > first:
             lax.fori_loop(first, last, lambda index, _: piece(index, False).start(), None)
@@ -404,7 +415,21 @@
         product = product + x5[other]
     x6[member] = (total + product).astype(jnp.bfloat16).astype(jnp.float32)
     arrive = side_swap(3, lambda other: x6.at[member], x6)
-    queue(piece_count)
+    queue(early_pieces)
+
+    hold = min(HOLD, chunk_count - early_chunks)
+    free_pieces = (chunk_count - hold) * (sections - 1)
+    holds = jnp.logical_not(late) & (section == 0)
+
+    @pl.when(jnp.logical_not(late))
+    def _():
+        lax.fori_loop(
+            early_pieces,
+            jnp.where(holds, free_pieces, piece_count),
+            lambda index, _: piece(index, False).start(),
+            None,
+        )
+
     arrive()
     for other in range(members):
         mixed_out[:, other * share : (other + 1) * share] = x6[other].astype(jnp.bfloat16)
@@ -412,6 +437,13 @@
     def place(chunk, _):
         for off in range(1, sections):
             piece(chunk * (sections - 1) + off - 1, True).wait_recv()
+
+        @pl.when(holds & (chunk == chunk_count - hold - TRIGGER))
+        def _():
+            lax.fori_loop(
+                free_pieces, piece_count, lambda index, _: piece(index, False).start(), None
+            )
+
         start = pl.multiple_of(chunk * CHUNK_ROWS, CHUNK_ROWS)
         for old in range(ROW_BLOCKS):
             first = old % per_section * block_rows
@@ -423,27 +455,153 @@
                 moved[places[block]]
             )
 
-    lax.fori_loop(0, chunk_count, place, None)
+    lax.fori_loop(0, chunks_here, place, None)
 
     for outgoing in sent:
         outgoing.wait_send()
-    lax.fori_loop(0, piece_count, lambda index, _: piece(index, False).wait_send(), None)
+    lax.fori_loop(
+        0,
+        chunks_here * (sections - 1),
+        lambda index, _: piece(index, False).wait_send(),
+        None,
+    )
+
+
+def rest_kernel(
+    sections,
+    early_chunks,
+    w_in,
+    order_in,
+    written_in,
+    new_out,
+    held,
+    order,
+    places,
+    moved,
+    load_sems,
+    bulk_send,
+    bulk_recv,
+):
+    replica = lax.axis_index("replica")
+    tp = lax.axis_index("tp")
+    sub = lax.axis_index("sub")
+    section = tp // PER_SECTION_TP
+    column = lax.rem(tp, PER_SECTION_TP)
+    rows_here, rows_old = held.shape[1:]
+    cols_dev = early_chunks * CHUNK_ROWS + rows_here
+    per_section = ROW_BLOCKS // sections
+    block_rows = rows_old // per_section
+    chunk_count = rows_here // CHUNK_ROWS
+    piece_count = chunk_count * (sections - 1)
+
+    def cross_peer(off):
+        other = lax.rem(section + off, sections)
+        return other, (replica, other * PER_SECTION_TP + column, sub)
+
+    def piece(index, arriving):
+        chunk = index // (sections - 1)
+        off = lax.rem(index, sections - 1) + 1
+        other, peer = cross_peer(off)
+        start = pl.multiple_of(chunk * CHUNK_ROWS, CHUNK_ROWS)
+        source = pl.multiple_of(
+            other * cols_dev + early_chunks * CHUNK_ROWS + start, CHUNK_ROWS
+        )
+        slot = lax.rem(section + sections - off, sections) if arriving else section
+        return pltpu.make_async_remote_copy(
+            src_ref=w_in.at[0, 0, pl.ds(source, CHUNK_ROWS)],
+            dst_ref=held.at[slot, pl.ds(start, CHUNK_ROWS)],
+            send_sem=bulk_send.at[index],
+            recv_sem=bulk_recv.at[index],
+            device_id=peer,
+            device_id_type=MESH,
+        )
+
+    def send(first, last):
+        lax.fori_loop(first, last, lambda index, _: piece(index, False).start(), None)
+
+    paced = section == sections - 1
+    lead = min(LEAD, chunk_count)
+
+    @pl.when(column >= PER_SECTION_TP // 2)
+    def _():
+        barrier = pltpu.get_barrier_semaphore()
+        for off in range(1, sections):
+            pl.semaphore_signal(barrier, inc=1, device_id=cross_peer(off)[1], device_id_type=MESH)
+        own_start = pl.multiple_of(section * cols_dev + early_chunks * CHUNK_ROWS, CHUNK_ROWS)
+        loads = [
+            pltpu.make_async_copy(order_in, order, load_sems.at[0]),
+            pltpu.make_async_copy(
+                w_in.at[0, 0, pl.ds(own_start, rows_here)], held.at[section], load_sems.at[1]
+            ),
+        ]
+        for load in loads:
+            load.start()
+        pl.semaphore_wait(barrier, sections - 1)
+        send(0, lead * (sections - 1))
+
+        @pl.when(jnp.logical_not(paced))
+        def _():
+            send(lead * (sections - 1), piece_count)
+
+        for load in loads:
+            load.wait()
+
+        def find(block, _):
+            place = jnp.int32(0)
+            for old in range(ROW_BLOCKS):
+                place = jnp.where(order[old] == block, old, place)
+            places[block] = place
+
+        lax.fori_loop(0, ROW_BLOCKS, find, None)
+
+        def place(chunk, _):
+            for off in range(1, sections):
+                piece(chunk * (sections - 1) + off - 1, True).wait_recv()
+
+            @pl.when(paced & (chunk + lead < chunk_count))
+            def _():
+                send((chunk + lead) * (sections - 1), (chunk + lead + 1) * (sections - 1))
+
+            start = pl.multiple_of(chunk * CHUNK_ROWS, CHUNK_ROWS)
+            for old in range(ROW_BLOCKS):
+                first = old % per_section * block_rows
+                moved[old] = held[
+                    old // per_section, pl.ds(start, CHUNK_ROWS), first : first + block_rows
+                ]
+            for block in range(ROW_BLOCKS):
+                new_out[
+                    0, 0, pl.ds(start, CHUNK_ROWS), block * block_rows : (block + 1) * block_rows
+                ] = moved[places[block]]
+
+        lax.fori_loop(0, chunk_count, place, None)
+        lax.fori_loop(0, piece_count, lambda index, _: piece(index, False).wait_send(), None)
 
 
 def written(mixed, new_weight):
-    rows = new_weight.shape[2] // WRITES
+    cols_dev = new_weight.shape[2]
+    early_rows = early_count(cols_dev // CHUNK_ROWS) * CHUNK_ROWS
 
     def kernel(mixed_ref, new_ref, mixed_out, new_out, sems):
-        copies = [pltpu.make_async_copy(mixed_ref, mixed_out, sems.at[WRITES])]
-        for index in range(WRITES):
-            part = (0, 0, pl.ds(index * rows, rows))
-            copies.append(
-                pltpu.make_async_copy(new_ref.at[part], new_out.at[part], sems.at[index])
-            )
-        for copy in copies:
-            copy.start()
-        for copy in copies:
-            copy.wait()
+        def copy(first, rows, index):
+            part = (0, 0, pl.ds(first, rows))
+            return pltpu.make_async_copy(new_ref.at[part], new_out.at[part], sems.at[index])
+
+        all_rows = lax.rem(lax.axis_index("tp"), PER_SECTION_TP) < PER_SECTION_TP // 2
+        copies = [
+            copy(0, early_rows, 0),
+            pltpu.make_async_copy(mixed_ref, mixed_out, sems.at[1]),
+        ]
+        for each in copies:
+            each.start()
+
+        @pl.when(all_rows)
+        def _():
+            late = copy(early_rows, cols_dev - early_rows, 2)
+            late.start()
+            late.wait()
+
+        for each in copies:
+            each.wait()
 
     return pl.pallas_call(
         kernel,
@@ -453,12 +611,37 @@
         ),
         in_specs=[pl.BlockSpec(memory_space=pltpu.VMEM)] * 2,
         out_specs=(pl.BlockSpec(memory_space=pltpu.HBM), pl.BlockSpec(memory_space=pltpu.HBM)),
-        scratch_shapes=[pltpu.SemaphoreType.DMA((WRITES + 1,))],
+        scratch_shapes=[pltpu.SemaphoreType.DMA((3,))],
         compiler_params=pltpu.CompilerParams(vmem_limit_bytes=2**20),
     )(
         pltpu.with_memory_space_constraint(mixed, pltpu.VMEM),
         pltpu.with_memory_space_constraint(new_weight, pltpu.VMEM),
     )
+
+
+def finished(new_weight, rest):
+    rows = rest.shape[2]
+    first = new_weight.shape[2] - rows
+
+    def kernel(new_ref, rest_ref, new_out, sem):
+        @pl.when(lax.rem(lax.axis_index("tp"), PER_SECTION_TP) >= PER_SECTION_TP // 2)
+        def _():
+            copy = pltpu.make_async_copy(rest_ref, new_out.at[:, :, pl.ds(first, rows)], sem)
+            copy.start()
+            copy.wait()
+
+    return pl.pallas_call(
+        kernel,
+        out_shape=jax.ShapeDtypeStruct(new_weight.shape, new_weight.dtype),
+        in_specs=[
+            pl.BlockSpec(memory_space=pltpu.HBM),
+            pl.BlockSpec(memory_space=pltpu.VMEM),
+        ],
+        out_specs=pl.BlockSpec(memory_space=pltpu.HBM),
+        scratch_shapes=[pltpu.SemaphoreType.DMA],
+        input_output_aliases={0: 0},
+        compiler_params=pltpu.CompilerParams(vmem_limit_bytes=2**20),
+    )(new_weight, pltpu.with_memory_space_constraint(rest, pltpu.VMEM))
 
 
 def shards(hidden_in, norm_gain, wqkv_old, wo, key_cache, value_cache, lengths, section_order):
@@ -544,7 +727,39 @@
             section_order,
         )
     with jax.named_scope("written"):
-        return written(*results)
+        mixed, new_weight = written(*results)
+    early_chunks = early_count(cols_dev // CHUNK_ROWS)
+    rest_rows = cols_dev - early_chunks * CHUNK_ROWS
+    rest_pieces = rest_rows // CHUNK_ROWS * (sections - 1)
+
+    def late_kernel(*refs):
+        rest_kernel(sections, early_chunks, *refs)
+
+    with jax.named_scope("rest"):
+        rest = pl.pallas_call(
+            late_kernel,
+            out_shape=pltpu.VMEM((1, 1, rest_rows, width), bf16),
+            in_specs=[pl.BlockSpec(memory_space=pltpu.HBM)] * 3,
+            out_specs=pl.BlockSpec(memory_space=pltpu.VMEM),
+            scratch_shapes=[
+                pltpu.VMEM((sections, rest_rows, rows_old), bf16),
+                pltpu.SMEM(section_order.shape, jnp.int32),
+                pltpu.SMEM(section_order.shape, jnp.int32),
+                pltpu.VMEM((ROW_BLOCKS, CHUNK_ROWS, block_rows), bf16),
+                pltpu.SemaphoreType.DMA((2,)),
+                pltpu.SemaphoreType.DMA((rest_pieces,)),
+                pltpu.SemaphoreType.DMA((rest_pieces,)),
+            ],
+            compiler_params=pltpu.CompilerParams(
+                collective_id=1, has_side_effects=True, vmem_limit_bytes=16 * 2**20
+            ),
+        )(
+            pltpu.with_memory_space_constraint(wqkv_old, pltpu.HBM),
+            pltpu.with_memory_space_constraint(section_order, pltpu.HBM),
+            pltpu.with_memory_space_constraint(mixed, pltpu.HBM),
+        )
+    with jax.named_scope("finished"):
+        return mixed, finished(new_weight, rest)
 
 
 def solution(mesh):

time: 239 us -> 235 us (0.983)
  Pallas kernels: 236 us -> 233 us
    pallas_call x1, Pallas kernels: 232 us -> 187 us  [shards(): pl.pallas_call(kernel, out_shape=(pltpu.VMEM((seqs, width), bf16), pltpu....]
    pallas_call x0 -> x2, Pallas kernels: none -> 42.5 us  [the longest x1 40.9 us: shards(): pl.pallas_call(late_kernel, out_shape=pltpu.VMEM((1, 1, rest_rows, width)...]
where the time goes in v3:
time: 235 us; the launch traced here: 234 us
  Pallas kernels  233 us (99%)
    pallas_call x1, Pallas kernels, shards(): pl.pallas_call(kernel, out_shape=(pltpu.VMEM((seqs, width), bf16), pltpu....  187 us
    pallas_call x1, Pallas kernels, shards(): pl.pallas_call(late_kernel, out_shape=pltpu.VMEM((1, 1, rest_rows, width)...  40.9 us

profile of v3, /device:TPU:27, one launch (start us, length us, event | category | flops | bytes accessed | tf_op | source)
XLA Modules:
  0.0 233.7 jit_solution(7270171715885300704)
XLA Ops:
  0.6 187.4 %layer.1 = (bf16[4,8192]{1,0:T(4,128)(2,1)S(1)}, bf16[1,1,640,8192]{3,2,1,0:T(8,128)(2,1)S(1)}) custom-call(bf16[4,8192]{1,0:T(4,128)(2,1)} %refs_0_.2, f32[1,8192]{1,0:T(1,128)} %bitcast.1, bf16[1,1,1280,4096]{3,2,1,0:T(8,128)(2,1)} %refs_0_.3, bf16[512,8192]{1,0:T(8,128)(2,1)} %refs_3_.1, bf16[4,256,1024]{2,1,0:T(8,128)(2,1)} %refs_4_.1, ...), custom_call_target="tpu_custom_call" | custom-call | tf_op jit(solution)/shard_map/layer/pallas_call | solution.py:707
  188.1 3.1 %written.1 = (bf16[4,8192]{1,0:T(4,128)(2,1)}, bf16[1,1,640,8192]{3,2,1,0:T(8,128)(2,1)}) custom-call(bf16[4,8192]{1,0:T(4,128)(2,1)S(1)} %get-tuple-element.6.mixed_ref, bf16[1,1,640,8192]{3,2,1,0:T(8,128)(2,1)S(1)} %get-tuple-element.7.new_ref), custom_call_target="tpu_custom_call" | custom-call | tf_op jit(solution)/shard_map/written/pallas_call | solution.py:606
  191.2 40.9 %rest.1.rest_ref = bf16[1,1,192,8192]{3,2,1,0:T(8,128)(2,1)S(1)} custom-call(bf16[1,1,1280,4096]{3,2,1,0:T(8,128)(2,1)} %refs_0_.3, s32[16]{0:T(128)} %refs_1_.1, bf16[4,8192]{1,0:T(4,128)(2,1)} %get-tuple-element.4.refs_2_), custom_call_target="tpu_custom_call" | custom-call | tf_op jit(solution)/shard_map/rest/pallas_call | solution.py:739
  232.0 1.7 finished.1
